TPU v7x, 256 devices: a whole 4x4x8 slice. The times are simulated.
256 devices in a mesh: dp: 64 (over z, y, core), tp: 4 (over x).
Axes of the slice: x: 4, y: 4, z: 8, core: 2. Of those that a mesh axis runs over, the one named last changes fastest.
Arguments:
- partial_up: bfloat16 [64, 1024, 4096], P('dp', None, 'tp'), may hold values from -8 to 8
- partial_down: bfloat16 [64, 4096, 1024], P('dp', 'tp'), may hold values from -8 to 8
- partial_norm: bfloat16 [64, 1024], P('dp'), may hold values from -16 to 16
- master_up: float32 [1024, 4096], P('dp', 'tp'), may hold values from -0.5 to 0.5
- master_down: float32 [4096, 1024], P('tp', 'dp'), may hold values from -0.25 to 0.25
- master_norm: float32 [1024], P('dp'), may hold values from 0.25 to 1.75
- memory_up: float32 [1024, 4096], P('dp', 'tp'), may hold values from 0.0001953125 to 0.001953125
- memory_down: float32 [4096, 1024], P('tp', 'dp'), may hold values from 4.8828126e-05 to 0.00048828125
- memory_norm: float32 [1024], P('dp'), may hold values from 0.05 to 0.8
Outputs:
- compute_up: bfloat16 [1024, 4096], P(None, 'tp')
- compute_down: bfloat16 [4096, 1024], P('tp')
- compute_norm: bfloat16 [1024], replicated
- stepped_up: float32 [1024, 4096], P('dp', 'tp')
- stepped_down: float32 [4096, 1024], P('tp', 'dp')
- stepped_norm: float32 [1024], P('dp')
- state_new_up: float32 [1024, 4096], P('dp', 'tp')
- state_new_down: float32 [4096, 1024], P('tp', 'dp')
- state_new_norm: float32 [1024], P('dp')
All inputs are finite; a program needn't handle non-finite values.
Results may differ from a plain program's by a relative error of at most 0.001.
Values may be sent and summed in bfloat16 or wider, within the bound.
A program may use at most 64 MiB of HBM per device.

v0:
```python
import jax
import jax.numpy as jnp
from jax import lax
from jax.sharding import Mesh
from jax.sharding import PartitionSpec as P

DP = ("dp_0", "dp_1", "dp_2")
learn_rate = 0.025
hold_rate = 0.8


def cut_along(array, dim, size):
    before, after = (array.shape[:dim], array.shape[dim + 1 :])
    return jnp.moveaxis(array.reshape(*before, size, -1, *after), dim, 0)


def sum_packed(arrays, axis, dims):
    size = lax.axis_size(axis)
    pieces = [cut_along(a, dim, size) for a, dim in zip(arrays, dims)]
    lines = jnp.concatenate([b.reshape(size, -1) for b in pieces], axis=1)
    width = max(16, -(-lines.shape[1] // 1024) * 8)
    lines = jnp.pad(lines, ((0, 0), (0, width * 128 - lines.shape[1]))).reshape(-1, 128)
    vector, at, gathered = (lax.psum_scatter(lines, axis, tiled=True).reshape(-1), 0, [])
    for b in pieces:
        part = b[0]
        gathered.append(vector[at : at + part.size].reshape(part.shape))
        at += part.size
    return tuple(gathered)


def over_axes(array, axes):
    for axis in axes:
        array = lax.psum(array, axis)
    return array


def sent_to_all(array, axis):
    copies = jnp.broadcast_to(array, (lax.axis_size(axis), *array.shape))
    return lax.all_to_all(copies, axis, split_axis=0, concat_axis=0, tiled=True)


def of_everyone(array, axis):
    everything = sent_to_all(array, axis)
    return jnp.sum(everything, axis=0)


def in_one(arrays, axis):
    ends = [0]
    for a in arrays:
        ends.append(ends[-1] + a.size)
    running = of_everyone(jnp.concatenate([a.ravel() for a in arrays]), axis)
    return tuple((running[b:e].reshape(a.shape) for a, b, e in zip(arrays, ends, ends[1:])))


def turned_gather(arrays, axis, dims):
    turned = [jnp.moveaxis(a, dim, 0) for a, dim in zip(arrays, dims)]
    widths = [t[0].size for t in turned]
    both = jnp.concatenate([t.reshape(-1, w) for t, w in zip(turned, widths)], axis=1)
    filled = lax.all_gather(both, axis, axis=0, tiled=True)
    pieces = jnp.split(filled, [sum(widths[:k]) for k in range(1, len(widths))], axis=1)
    return tuple(
        (
            jnp.moveaxis(b.reshape(-1, *t.shape[1:]), 0, dim)
            for b, t, dim in zip(pieces, turned, dims)
        )
    )


def local(
    partial_up,
    partial_down,
    partial_norm,
    master_up,
    master_down,
    master_norm,
    memory_up,
    memory_down,
    memory_norm,
):
    mean_up, mean_down = sum_packed(
        (partial_up[0].astype(jnp.float32), partial_down[0].astype(jnp.float32)), DP, (0, 1)
    )
    whole_norm = over_axes(partial_norm[0].astype(jnp.float32), DP)
    place = lax.axis_index(DP)
    mean_norm = lax.dynamic_slice_in_dim(
        whole_norm, place * master_norm.shape[0], master_norm.shape[0]
    )
    mean_rate = lax.axis_size(DP) ** (-0.5)
    mean_up = mean_up * mean_rate
    mean_down = mean_down * mean_rate
    mean_norm = mean_norm * mean_rate
    own_up, own_down, slope_up_norm, slope_down_norm = in_one(
        (
            jnp.sum(master_up * master_up, axis=1, keepdims=True),
            jnp.sum(master_down * master_down, axis=0, keepdims=True),
            jnp.sum(mean_up * mean_up, axis=1, keepdims=True),
            jnp.sum(mean_down * mean_down, axis=0, keepdims=True),
        ),
        "tp",
    )
    mean_up = mean_up * (jnp.sqrt(own_up) * lax.rsqrt(slope_up_norm + 1e-06))
    mean_down = mean_down * (jnp.sqrt(own_down) * lax.rsqrt(slope_down_norm + 1e-06))
    state_new_up = hold_rate * memory_up + (1.0 - hold_rate) * mean_up * mean_up
    stepped_up = master_up - learn_rate * mean_up * lax.rsqrt(state_new_up + 1e-06)
    state_new_down = hold_rate * memory_down + (1.0 - hold_rate) * mean_down * mean_down
    stepped_down = master_down - learn_rate * mean_down * lax.rsqrt(state_new_down + 1e-06)
    state_new_norm = hold_rate * memory_norm + (1.0 - hold_rate) * mean_norm * mean_norm
    stepped_norm = master_norm - learn_rate * mean_norm * lax.rsqrt(state_new_norm + 1e-06)
    compute_up, compute_down, compute_norm = turned_gather(
        (
            stepped_up.astype(jnp.bfloat16),
            stepped_down.astype(jnp.bfloat16),
            stepped_norm.astype(jnp.bfloat16),
        ),
        DP,
        (0, 1, 0),
    )
    return (
        compute_up,
        compute_down,
        compute_norm,
        stepped_up,
        stepped_down,
        stepped_norm,
        state_new_up,
        state_new_down,
        state_new_norm,
    )


def solution(mesh):
    finer = Mesh(mesh.devices.reshape(8, 4, 2, mesh.shape["tp"]), ("dp_0", "dp_1", "dp_2", "tp"))
    return jax.shard_map(
        local,
        mesh=finer,
        in_specs=(
            P(DP, None, "tp"),
            P(DP, "tp", None),
            P(DP, None),
            P(DP, "tp"),
            P("tp", DP),
            P(DP),
            P(DP, "tp"),
            P("tp", DP),
            P(DP),
        ),
        out_specs=(
            P(None, "tp"),
            P("tp", None),
            P(),
            P(DP, "tp"),
            P("tp", DP),
            P(DP),
            P(DP, "tp"),
            P("tp", DP),
            P(DP),
        ),
        check_vma=False,
    )
```

profile of v0, /device:TPU:1, one launch (start us, length us, event | category | flops | bytes accessed | tf_op | source)
XLA Modules:
  0.0 300.1 jit_solution(11367496237568048185)
XLA Ops:
  7.2 2.9 copy.45
  10.1 6.1 %copy.46 = bf16[64,1024,16]{0,2,1:T(8,128)(2,1)} copy(bf16[64,1024,16]{1,2,0:T(8,128)(2,1)S(1)} %bitcast.13) | data formatting | bytes 4194304 | tf_op jit(solution)/shard_map/transpose | solution.py:14
  16.2 3.5 %copy.47 = bf16[64,16384]{1,0:T(8,128)(2,1)S(1)} copy(bf16[64,16384]{0,1:T(8,128)(2,1)} %bitcast.12) | data formatting | bytes 4194304 | tf_op jit(solution)/shard_map/reshape | solution.py:20
  19.8 4.2 %convert_element_type.25 = bf16[64,16384]{1,0:T(8,128)(2,1)} reshape(bf16[1,1024,1024]{2,1,0:T(8,128)(2,1)} %param.9) | data formatting | bytes 4194304 | tf_op jit(solution)/shard_map/convert_element_type | solution.py:81
  23.9 5.3 %maximum_convert_fusion = f32[64,32768]{1,0:T(8,128)} fusion(bf16[64,16384]{1,0:T(8,128)(2,1)S(1)} %copy.47, bf16[64,16384]{1,0:T(8,128)(2,1)} %convert_element_type.25), kind=kLoop, calls=%fused_computation | loop fusion | flops 8388608 | bytes 12582912 | tf_op jit(solution)/shard_map/reshape | solution.py:22
  29.3 9.3 %reshape.81 = f32[16384,128]{1,0:T(8,128)} reshape(f32[64,32768]{1,0:T(8,128)} %maximum_convert_fusion) | data formatting | bytes 16777216 | tf_op jit(solution)/shard_map/reshape | solution.py:22
  38.7 0.6 copy-done.4
  39.3 17.3 %psum.21 = f32[1024]{0:T(1024)S(1)} all-reduce(f32[1024]{0:T(1024)S(1)} %bitcast.14), channel_id=1, replica_groups=mesh['dp_0'=8,'dp_1'=4,'dp_2'=2,'tp'=4] {'dp_0'}, use_global_device_ids=true, to_apply=%region_7.8 | all-reduce | flops 1024 | bytes 8192 | tf_op jit(solution)/shard_map/psum | solution.py:33
  56.6 8.7 %psum.22 = f32[1024]{0:T(1024)S(1)} all-reduce(f32[1024]{0:T(1024)S(1)} %psum.21), channel_id=1, replica_groups=mesh['dp_0'=8,'dp_1'=4,'dp_2'=2,'tp'=4] {'dp_1'}, use_global_device_ids=true, to_apply=%region_8.9 | all-reduce | flops 1024 | bytes 8192 | tf_op jit(solution)/shard_map/psum | solution.py:33
  65.3 8.3 %psum.23 = f32[1024]{0:T(1024)S(1)} all-reduce(f32[1024]{0:T(1024)S(1)} %psum.22), channel_id=1, replica_groups=mesh['dp_0'=8,'dp_1'=4,'dp_2'=2,'tp'=4] {'dp_2'}, use_global_device_ids=true, to_apply=%region_9.10 | all-reduce | flops 1024 | bytes 8192 | tf_op jit(solution)/shard_map/psum | solution.py:33
  73.9 116.3 %reduce-scatter.2.cloned.1.call-done = f32[256,128]{1,0:T(8,128)} async-done(((f32[16384,128]{1,0:T(8,128)}), f32[256,128]{1,0:T(8,128)}) %reduce-scatter.2.cloned.1.call-update) | async-done | bytes 131088 | tf_op jit(solution)/shard_map/reduce_scatter | solution.py:23
  190.1 1.0 fusion.5
  191.1 0.2 reshape.77
  191.7 0.6 broadcast_in_dim.3
  192.3 4.4 %all-to-all-start = ((f32[4,1,64]{2,1,0:T(1,128)}), f32[4,1,64]{2,1,0:T(1,128)S(1)}, u32[]{:S(2)}, u32[]{:S(2)}) async-start(f32[4,1,64]{2,1,0:T(1,128)} %broadcast_in_dim.3), calls=%async_computation.1 | async-start | bytes 4096 | tf_op jit(solution)/shard_map/all_to_all | solution.py:39
  196.7 0.6 convert_bitcast_fusion.1
  197.6 3.2 %all-to-all-done = f32[4,1,64]{2,1,0:T(1,128)S(1)} async-done(((f32[4,1,64]{2,1,0:T(1,128)}), f32[4,1,64]{2,1,0:T(1,128)S(1)}, u32[]{:S(2)}, u32[]{:S(2)}) %all-to-all-start) | async-done | bytes 1056 | tf_op jit(solution)/shard_map/all_to_all | solution.py:39
  200.9 0.7 convert_bitcast_fusion
  201.6 0.7 fusion.2
  202.4 0.6 pad_maximum_fusion
  203.0 82.0 %all-gather.2.cloned.1.call-done = bf16[1024,2049]{1,0:T(8,128)(2,1)} async-done(((bf16[16,2049]{1,0:T(8,128)(2,1)}), bf16[1024,2049]{1,0:T(8,128)(2,1)}) %all-gather.2.cloned.1.call-update) | async-done | bytes 4196368 | tf_op jit(solution)/shard_map/all_gather | solution.py:59
  285.0 4.0 %slice_bitcast_fusion = (bf16[1024,1024]{0,1:T(8,128)(2,1)S(1)}, bf16[1024,1024]{1,0:T(8,128)(2,1)}) fusion(bf16[1024,2049]{1,0:T(8,128)(2,1)} %all-gather.2.cloned.1.call-done), kind=kLoop, calls=%fused_computation.1 | loop fusion | bytes 8388608 | tf_op jit(solution)/shard_map/transpose | solution.py:63
  289.0 2.5 copy.51
  291.6 1.7 slice_reduce_fusion
  (29 shorter events, 1.2 us)
Async XLA Ops:
  7.2 183.0 %reduce-scatter.2.cloned.1.call-start = ((), (), s32[]{:S(2)}) async-start(), calls=%async_computation.2 | async-start | bytes 8519680 | tf_op jit(solution)/shard_map/reduce_scatter | solution.py:23
  38.6 0.7 copy-start.4
  38.6 35.0 %copy-start = (f32[1024,16]{0,1:T(8,128)S(1)}, f32[1024,16]{0,1:T(8,128)}, u32[]{:S(2)}) copy-start(f32[1024,16]{0,1:T(8,128)} %param.13) | copy-start | bytes 196612
  38.6 35.2 %copy-start.1 = (f32[16,1024]{1,0:T(8,128)S(1)}, f32[16,1024]{1,0:T(8,128)}, u32[]{:S(2)}) copy-start(f32[16,1024]{1,0:T(8,128)} %param.12) | copy-start | bytes 196612
  38.6 158.1 %copy-start.5 = (f32[16]{0:T(128)S(1)}, f32[16]{0:T(128)}, u32[]{:S(2)}) copy-start(f32[16]{0:T(128)} %param.14) | copy-start | bytes 196
  38.6 158.1 %copy-start.6 = (f32[16]{0:T(128)S(1)}, f32[16]{0:T(128)}, u32[]{:S(2)}) copy-start(f32[16]{0:T(128)} %param.17) | copy-start | bytes 196
  38.6 162.3 %copy-start.2 = (f32[1024,16]{0,1:T(8,128)S(1)}, f32[1024,16]{0,1:T(8,128)}, u32[]{:S(2)}) copy-start(f32[1024,16]{0,1:T(8,128)} %param.16) | copy-start | bytes 196612
  38.6 163.0 %copy-start.3 = (f32[16,1024]{1,0:T(8,128)S(1)}, f32[16,1024]{1,0:T(8,128)}, u32[]{:S(2)}) copy-start(f32[16,1024]{1,0:T(8,128)} %param.15) | copy-start | bytes 196612
  192.3 8.4 %all-to-all-start = ((f32[4,1,64]{2,1,0:T(1,128)}), f32[4,1,64]{2,1,0:T(1,128)S(1)}, u32[]{:S(2)}, u32[]{:S(2)}) async-start(f32[4,1,64]{2,1,0:T(1,128)} %broadcast_in_dim.3), calls=%async_computation.1 | async-start | bytes 4096 | tf_op jit(solution)/shard_map/all_to_all | solution.py:39
  196.7 88.3 %all-gather.2.cloned.1.call-start = ((), (), s32[]{:S(2)}) async-start(), calls=%async_computation.3 | async-start | bytes 4526080 | tf_op jit(solution)/shard_map/all_gather | solution.py:59
Sparse Core Ops, SparseCore 0:
  38.8 151.3 reduce-scatter.1
  203.1 81.8 all-gather.1
where the time goes:
time: 301 us; the launch traced here: 300 us
  waiting for transfers between devices  201 us (67%)
  local copies, waits for them, and re-layouts  36 us (12%)
  blocking collectives  34.4 us (11%)
  between operations  14.1 us (5%)
  other arithmetic  9.73 us (3%)
  starting transfers between devices  4.42 us (1%)
    reduce_scatter x1, waiting for transfers between devices, sum_packed(): lax.psum_scatter(lines, axis, tiled=True).reshape(-1)  116 us
    all_gather x1, waiting for transfers between devices, turned_gather(): filled = lax.all_gather(both, axis, axis=0, tiled=True)  82 us
    psum x3, blocking collectives, over_axes(): array = lax.psum(array, axis)  34.4 us
    reshape x1, local copies, waits for them, and re-layouts, sum_packed(): jnp.pad(lines, ((0, 0), (0, width * 128 - lines.shape[1]))).reshape(-1, 128)  9.28 us
    transpose x1, local copies, waits for them, and re-layouts, cut_along(): return jnp.moveaxis(array.reshape(*before, size, -1, *after), dim, 0)  6.13 us
    unnamed x16, local copies, waits for them, and re-layouts  6.03 us
  transfers between devices with their start and end apart: 3, of which 3 were waited for; matrix products, arithmetic and copies ran while one was open for 0% of the time, Pallas kernels for 0%

commit v1 on v0

--- a/solution.py
+++ b/solution.py
@@ -56,7 +56,9 @@
     turned = [jnp.moveaxis(a, dim, 0) for a, dim in zip(arrays, dims)]
     widths = [t[0].size for t in turned]
     both = jnp.concatenate([t.reshape(-1, w) for t, w in zip(turned, widths)], axis=1)
-    filled = lax.all_gather(both, axis, axis=0, tiled=True)
+    filled = jnp.concatenate(
+        lax.all_to_all(jnp.stack([both] * lax.axis_size(axis)), axis, 0, 0), axis=0
+    )
     pieces = jnp.split(filled, [sum(widths[:k]) for k in range(1, len(widths))], axis=1)
     return tuple(
         (

time: 301 us -> 332 us (1.10)
  blocking collectives: 34.4 us -> 151 us
  waiting for transfers between devices: 201 us -> 119 us
    all_to_all x0 -> x1, blocking collectives: none -> 116 us  [turned_gather(): lax.all_to_all(jnp.stack([both] * lax.axis_size(axis)), axis, 0, 0)]
    all_gather x1 -> x0, waiting for transfers between devices: 82 us -> none  [turned_gather(): filled = lax.all_gather(both, axis, axis=0, tiled=True)]
  transfers between devices with their start and end apart: 3 -> 2, of which waited for: 3 -> 2; matrix products, arithmetic and copies ran while one was open for 0% -> 0% of each run, Pallas kernels for 0% -> 0%
where the time goes in v1:
time: 332 us; the launch traced here: 331 us
  blocking collectives  151 us (45%)
  waiting for transfers between devices  119 us (36%)
  local copies, waits for them, and re-layouts  33.3 us (10%)
  between operations  14.1 us (4%)
  other arithmetic  9.1 us (3%)
  starting transfers between devices  4.42 us (1%)
    all_to_all x1, blocking collectives, turned_gather(): lax.all_to_all(jnp.stack([both] * lax.axis_size(axis)), axis, 0, 0)  116 us
    reduce_scatter x1, waiting for transfers between devices, sum_packed(): lax.psum_scatter(lines, axis, tiled=True).reshape(-1)  116 us
    psum x3, blocking collectives, over_axes(): array = lax.psum(array, axis)  34.4 us
    reshape x1, local copies, waits for them, and re-layouts, sum_packed(): jnp.pad(lines, ((0, 0), (0, width * 128 - lines.shape[1]))).reshape(-1, 128)  9.28 us
  transfers between devices with their start and end apart: 2, of which 2 were waited for; matrix products, arithmetic and copies ran while one was open for 0% of the time, Pallas kernels for 0%

profile of v1, /device:TPU:1, one launch (start us, length us, event | category | flops | bytes accessed | tf_op | source)
XLA Modules:
  0.0 331.1 jit_solution(3168704832149935460)
XLA Ops:
  7.2 2.9 copy.47
  10.1 6.1 %copy.48 = bf16[64,1024,16]{0,2,1:T(8,128)(2,1)} copy(bf16[64,1024,16]{1,2,0:T(8,128)(2,1)S(1)} %bitcast.16) | data formatting | bytes 4194304 | tf_op jit(solution)/shard_map/transpose | solution.py:14
  16.2 3.5 %copy.49 = bf16[64,16384]{1,0:T(8,128)(2,1)S(1)} copy(bf16[64,16384]{0,1:T(8,128)(2,1)} %bitcast.15) | data formatting | bytes 4194304 | tf_op jit(solution)/shard_map/reshape | solution.py:20
  19.8 4.2 %convert_element_type.25 = bf16[64,16384]{1,0:T(8,128)(2,1)} reshape(bf16[1,1024,1024]{2,1,0:T(8,128)(2,1)} %param.9) | data formatting | bytes 4194304 | tf_op jit(solution)/shard_map/convert_element_type | solution.py:83
  23.9 5.3 %maximum_convert_fusion = f32[64,32768]{1,0:T(8,128)} fusion(bf16[64,16384]{1,0:T(8,128)(2,1)S(1)} %copy.49, bf16[64,16384]{1,0:T(8,128)(2,1)} %convert_element_type.25), kind=kLoop, calls=%fused_computation | loop fusion | flops 8388608 | bytes 12582912 | tf_op jit(solution)/shard_map/reshape | solution.py:22
  29.3 9.3 %reshape.87 = f32[16384,128]{1,0:T(8,128)} reshape(f32[64,32768]{1,0:T(8,128)} %maximum_convert_fusion) | data formatting | bytes 16777216 | tf_op jit(solution)/shard_map/reshape | solution.py:22
  38.7 0.6 copy-done.4
  39.3 17.3 %psum.21 = f32[1024]{0:T(1024)S(1)} all-reduce(f32[1024]{0:T(1024)S(1)} %bitcast.17), channel_id=1, replica_groups=mesh['dp_0'=8,'dp_1'=4,'dp_2'=2,'tp'=4] {'dp_0'}, use_global_device_ids=true, to_apply=%region_7.8 | all-reduce | flops 1024 | bytes 8192 | tf_op jit(solution)/shard_map/psum | solution.py:33
  56.6 8.7 %psum.22 = f32[1024]{0:T(1024)S(1)} all-reduce(f32[1024]{0:T(1024)S(1)} %psum.21), channel_id=1, replica_groups=mesh['dp_0'=8,'dp_1'=4,'dp_2'=2,'tp'=4] {'dp_1'}, use_global_device_ids=true, to_apply=%region_8.9 | all-reduce | flops 1024 | bytes 8192 | tf_op jit(solution)/shard_map/psum | solution.py:33
  65.3 8.3 %psum.23 = f32[1024]{0:T(1024)S(1)} all-reduce(f32[1024]{0:T(1024)S(1)} %psum.22), channel_id=1, replica_groups=mesh['dp_0'=8,'dp_1'=4,'dp_2'=2,'tp'=4] {'dp_2'}, use_global_device_ids=true, to_apply=%region_9.10 | all-reduce | flops 1024 | bytes 8192 | tf_op jit(solution)/shard_map/psum | solution.py:33
  73.9 116.3 %reduce-scatter.2.cloned.1.call-done = f32[256,128]{1,0:T(8,128)} async-done(((f32[16384,128]{1,0:T(8,128)}), f32[256,128]{1,0:T(8,128)}) %reduce-scatter.2.cloned.1.call-update) | async-done | bytes 131088 | tf_op jit(solution)/shard_map/reduce_scatter | solution.py:23
  190.1 1.0 fusion.5
  191.1 0.2 reshape.82
  191.7 0.6 broadcast_in_dim.3
  192.3 4.4 %all-to-all-start = ((f32[4,1,64]{2,1,0:T(1,128)}), f32[4,1,64]{2,1,0:T(1,128)S(1)}, u32[]{:S(2)}, u32[]{:S(2)}) async-start(f32[4,1,64]{2,1,0:T(1,128)} %broadcast_in_dim.3), calls=%async_computation.1 | async-start | bytes 4096 | tf_op jit(solution)/shard_map/all_to_all | solution.py:39
  196.7 0.6 convert_bitcast_fusion.1
  197.6 3.2 all-to-all-done
  200.9 0.7 convert_bitcast_fusion
  201.6 0.7 fusion.2
  202.4 0.3 stack.2
  202.7 116.4 %all_to_all.11 = bf16[64,16,2049]{2,1,0:T(8,128)(2,1)S(1)} all-to-all(bf16[64,16,2049]{2,1,0:T(8,128)(2,1)S(1)} %stack.2), channel_id=1, replica_groups=mesh['dp_0'=8,'dp_1'=4,'dp_2'=2,'tp'=4] {'dp_0','dp_1','dp_2'}, dimensions={0} | all-to-all | bytes 8392704 | tf_op jit(solution)/shard_map/all_to_all | solution.py:60
  319.1 1.9 slice_bitcast_fusion
  321.0 0.7 slice_reduce_fusion
  321.7 2.5 copy.53
  (28 shorter events, 1.1 us)
Async XLA Ops:
  7.2 183.0 %reduce-scatter.2.cloned.1.call-start = ((), (), s32[]{:S(2)}) async-start(), calls=%async_computation.3 | async-start | bytes 8519680 | tf_op jit(solution)/shard_map/reduce_scatter | solution.py:23
  38.6 0.7 copy-start.4
  38.6 35.0 %copy-start = (f32[1024,16]{0,1:T(8,128)S(1)}, f32[1024,16]{0,1:T(8,128)}, u32[]{:S(2)}) copy-start(f32[1024,16]{0,1:T(8,128)} %param.13) | copy-start | bytes 196612
  38.6 35.2 %copy-start.1 = (f32[16,1024]{1,0:T(8,128)S(1)}, f32[16,1024]{1,0:T(8,128)}, u32[]{:S(2)}) copy-start(f32[16,1024]{1,0:T(8,128)} %param.12) | copy-start | bytes 196612
  38.6 158.1 %copy-start.5 = (f32[16]{0:T(128)S(1)}, f32[16]{0:T(128)}, u32[]{:S(2)}) copy-start(f32[16]{0:T(128)} %param.14) | copy-start | bytes 196
  38.6 158.1 %copy-start.6 = (f32[16]{0:T(128)S(1)}, f32[16]{0:T(128)}, u32[]{:S(2)}) copy-start(f32[16]{0:T(128)} %param.17) | copy-start | bytes 196
  38.6 162.3 %copy-start.2 = (f32[1024,16]{0,1:T(8,128)S(1)}, f32[1024,16]{0,1:T(8,128)}, u32[]{:S(2)}) copy-start(f32[1024,16]{0,1:T(8,128)} %param.16) | copy-start | bytes 196612
  38.6 163.0 %copy-start.3 = (f32[16,1024]{1,0:T(8,128)S(1)}, f32[16,1024]{1,0:T(8,128)}, u32[]{:S(2)}) copy-start(f32[16,1024]{1,0:T(8,128)} %param.15) | copy-start | bytes 196612
  192.3 8.4 %all-to-all-start = ((f32[4,1,64]{2,1,0:T(1,128)}), f32[4,1,64]{2,1,0:T(1,128)S(1)}, u32[]{:S(2)}, u32[]{:S(2)}) async-start(f32[4,1,64]{2,1,0:T(1,128)} %broadcast_in_dim.3), calls=%async_computation.1 | async-start | bytes 4096 | tf_op jit(solution)/shard_map/all_to_all | solution.py:39
Sparse Core Ops, SparseCore 0:
  38.8 151.3 reduce-scatter.1
